TPU v7x, 8 devices: a whole 2x2x1 slice. The times are simulated.
8 devices in a mesh: data: 1 (over z), row: 2 (over y), col: 4 (over x, core).
Axes of the slice: x: 2, y: 2, z: 1, core: 2. Of those that a mesh axis runs over, the one named last changes fastest.
Arguments:
- tokens: bfloat16 [1536, 2048], P(('data', 'row', 'col'))
- expert_ids: int32 [1536, 8], P(('data', 'row', 'col'))
- gate_weights: float32 [1536, 8], P(('data', 'row', 'col'))
- w_in: bfloat16 [64, 2048, 1024], P(('row', 'col'))
- w_out: bfloat16 [64, 1024, 2048], P(('row', 'col'))
Outputs:
- output: bfloat16 [1536, 2048], P(('data', 'row', 'col'))
All inputs are finite; a program needn't handle non-finite values.
Results may differ from a plain program's by a relative error of at most 0.00449034.
Values are sent between devices in bfloat16 or wider.
A program may use at most 1 GiB of HBM per device.

v0:
```python
import jax
import jax.numpy as jnp
from jax import lax
from jax.sharding import PartitionSpec as P

GRID_AXES = ('row', 'col')


def local_ranks(flat_ids, num_experts):
    pair_count = flat_ids.shape[0]
    sort_order = jnp.argsort(flat_ids, stable=True)
    counts = jnp.zeros((num_experts,), jnp.int32).at[flat_ids].add(1)
    starts = jnp.cumsum(counts) - counts
    sorted_rank = jnp.arange(pair_count, dtype=jnp.int32) - starts[flat_ids[sort_order]]
    pair_rank = jnp.zeros((pair_count,), jnp.int32).at[sort_order].set(sorted_rank)
    return counts, pair_rank


def solution(mesh):
    rows_n = mesh.shape['row']
    cols_n = mesh.shape['col']
    group_size = rows_n * cols_n

    def device_fn(tokens, expert_ids, gate_weights, w_in, w_out):
        tok_dev, model_width = tokens.shape
        top_k = expert_ids.shape[1]
        local_experts = w_in.shape[0]
        num_experts = local_experts * group_size
        capacity = tok_dev * group_size * top_k // num_experts
        per_source = 2 * tok_dev * top_k // num_experts
        flat_ids = expert_ids.reshape(-1)
        pair_count = flat_ids.shape[0]
        counts, pair_rank = local_ranks(flat_ids, num_experts)

        col_counts = lax.all_gather(counts, 'col')
        col_before = jnp.arange(cols_n)[:, None] < lax.axis_index('col')
        before_col = jnp.sum(jnp.where(col_before, col_counts, 0), axis=0)
        row_totals = lax.all_gather(jnp.sum(col_counts, axis=0), 'row')
        row_before = jnp.arange(rows_n)[:, None] < lax.axis_index('row')
        before_row = jnp.sum(jnp.where(row_before, row_totals, 0), axis=0)
        offsets = before_row + before_col

        global_rank = offsets[flat_ids] + pair_rank
        send_pos = flat_ids * per_source + pair_rank
        send_token = jnp.where(global_rank < capacity, jnp.arange(pair_count, dtype=jnp.int32) // top_k, tok_dev)
        send_index = jnp.full((num_experts * per_source,), tok_dev, jnp.int32).at[send_pos].set(send_token)
        send_rows = jnp.take(tokens, send_index, axis=0, mode='fill', fill_value=0)
        send_rows = send_rows.reshape(group_size, local_experts, per_source, model_width)
        meta_send = jnp.stack([offsets, counts], axis=-1).reshape(group_size, local_experts, 2)

        meta_recv = lax.all_to_all(meta_send, GRID_AXES, 0, 0, tiled=True)
        recv_rows = lax.all_to_all(send_rows, GRID_AXES, 0, 0, tiled=True)

        source_off = meta_recv[:, :, 0]
        source_cnt = meta_recv[:, :, 1]
        source_end = source_off + source_cnt
        slot_pos = jnp.arange(capacity)
        slot_source = jnp.sum(source_end.T[:, None, :] <= slot_pos[None, :, None], axis=-1)
        source_clip = jnp.minimum(slot_source, group_size - 1)
        slot_start = jnp.take_along_axis(source_off.T, source_clip, axis=1)
        expert_pos = jnp.arange(local_experts)[:, None]
        recv_index = (source_clip * local_experts + expert_pos) * per_source + slot_pos[None, :] - slot_start
        recv_index = jnp.where(slot_source < group_size, recv_index, group_size * local_experts * per_source)
        buffer = jnp.take(recv_rows.reshape(-1, model_width), recv_index.reshape(-1), axis=0, mode='fill', fill_value=0)
        buffer = buffer.reshape(local_experts, capacity, model_width)

        hidden = jax.nn.gelu(jnp.einsum('ecd,edf->ecf', buffer, w_in, preferred_element_type=jnp.float32)).astype(jnp.bfloat16)
        expert_out = jnp.einsum('ecf,efd->ecd', hidden, w_out, preferred_element_type=jnp.float32).astype(jnp.bfloat16)

        back_pos = jnp.arange(per_source)
        back_slot = source_off[:, :, None] + back_pos
        back_valid = (back_pos < source_cnt[:, :, None]) & (back_slot < capacity)
        back_index = jnp.where(back_valid, jnp.arange(local_experts)[None, :, None] * capacity + back_slot, local_experts * capacity)
        back_rows = jnp.take(expert_out.reshape(-1, model_width), back_index.reshape(-1), axis=0, mode='fill', fill_value=0)
        back_rows = back_rows.reshape(group_size, local_experts, per_source, model_width)
        returned = lax.all_to_all(back_rows, GRID_AXES, 0, 0, tiled=True)

        pair_rows = jnp.take(returned.reshape(-1, model_width), send_pos, axis=0, mode='fill', fill_value=0).reshape(tok_dev, top_k, model_width)
        mixed_sum = jnp.einsum('tk,tkd->td', gate_weights, pair_rows, preferred_element_type=jnp.float32)
        return (tokens.astype(jnp.float32) + mixed_sum).astype(jnp.bfloat16)

    token_spec = P(('data', 'row', 'col'), None)
    expert_spec = P(GRID_AXES, None, None)
    return jax.shard_map(device_fn, mesh=mesh, in_specs=(token_spec, token_spec, token_spec, expert_spec, expert_spec), out_specs=token_spec, check_vma=False)
```

profile of v0, /device:TPU:0, one launch (start us, length us, event | category | flops | bytes accessed | tf_op | source)
XLA Modules:
  0.0 574.2 jit_solution(18239736601521693499)
XLA Ops:
  0.0 0.9 copy.19
  0.9 0.1 reshape.274
  1.0 11.1 %scatter_custom_fusion = s32[64]{0:T(128)S(1)} fusion(s32[1536]{0:T(1024)S(1)} %fusion.31, s32[1536]{0:T(1024)S(1)} %broadcast.476, s32[]{:T(128)} %constant.48.clone.1), kind=kCustom, calls=%fused_computation.151 | custom fusion | flops 1536 | bytes 260 | tf_op jit(solution)/shard_map/scatter-add | solution.py:12
  12.3 1.2 dynamic-slice
  14.2 0.2 dynamic-update-slice
  14.4 6.8 %all-reduce = s32[256]{0:T(256)S(1)} all-reduce(s32[256]{0:T(256)S(1)} %dynamic-update-slice), channel_id=2, replica_groups=mesh['data'=1,'row'=2,'col'=4] {'col'}, use_global_device_ids=true, to_apply=%add | all-reduce | flops 256 | bytes 2048
  21.3 1.2 dynamic-slice.1
  23.2 0.2 dynamic-update-slice.1
  23.5 4.3 all-reduce.1
  28.0 0.6 copy.22
  28.6 2.0 all-to-all-start
  30.6 0.1 copy.21
  30.8 0.1 reduce.2
  30.9 0.7 fusion.50
  31.7 0.7 fusion.51
  32.3 0.1 reshape.275
  32.4 0.7 fusion.48
  33.2 0.7 fusion.49
  33.9 0.7 fusion.45
  34.6 0.7 fusion.46
  35.3 0.7 fusion.44
  36.1 0.7 fusion.47
  36.8 5.0 sort.17
  41.8 8.4 %gather_fusion = s32[1536]{0:T(1024)S(1)} fusion(s32[1536]{0:T(1024)S(1)} %reshape.275, s32[2048]{0:T(1024)S(1)} %pad_clamp_fusion.2), kind=kCustom, calls=%fused_computation.2 | custom fusion | bytes 18432 | tf_op jit(solution)/shard_map/gather | solution.py:14
  50.2 4.4 fusion.30
  54.6 1.1 compare_reduce_fusion.56
  55.8 35.6 %select_subtract_fusion = s32[1536]{0:T(1024)S(1)} fusion(pred[1536]{0:T(1024)(128)(4,1)S(1)} %get-tuple-element.64, pred[1536]{0:T(1024)(128)(4,1)S(1)} %get-tuple-element.63, pred[1536]{0:T(1024)(128)(4,1)S(1)} %get-tuple-element.62, pred[1536]{0:T(1024)(128)(4,1)S(1)} %get-tuple-element.61, pred[1536]{0:T(1024)(128)(4,1)S(1)} %get-tuple-element.60, ...), kind=kLoop, calls=%fused_computation.132 | loop fusion | flops 89088 | bytes 100068 | tf_op jit(solution)/shard_map/sub | solution.py:14
  91.3 6.2 %scatter_custom_fusion.1 = s32[1536]{0:T(1024)S(1)} fusion(s32[1536]{0:T(1024)S(1)} %compare_select_fusion.15, s32[1536]{0:T(1024)S(1)} %select_subtract_fusion, s32[]{:T(128)} %constant.48.clone.1), kind=kCustom, calls=%fused_computation.144 | custom fusion | bytes 6148 | tf_op jit(solution)/shard_map/scatter | solution.py:15
  97.5 0.6 compare_and_fusion.2
  98.1 39.9 %fusion.22 = s32[1536]{0:T(1024)S(1)} fusion(s32[1536]{0:T(1024)S(1)} %scatter_custom_fusion.1, s32[1536]{0:T(1024)S(1)} %fusion.31, s32[]{:T(128)} %bitcast.72, s32[]{:T(128)} %bitcast.73, s32[]{:T(128)} %bitcast.74, s32[]{:T(128)} %bitcast.75, s32[]{:T(128)} %bitcast.76, s32[]{:T(128)} %bitcast.77, s32[]{:T(128)} %bitcast.78, s32[]{:T(128)} %bitcast.79, ...), kind=kLoop, calls=%fused_computation.120 | loop fusion | flops 210432 | bytes 18688 | tf_op jit(solution)/shard_map/jit(_where)/select_n | solution.py:45
  138.1 6.2 %scatter_custom_fusion.2 = s32[3072]{0:T(1024)S(1)} fusion(s32[1536]{0:T(1024)S(1)} %get-tuple-element.68, s32[1536]{0:T(1024)S(1)} %fusion.22, s32[]{:T(128)} %constant.58.clone.1), kind=kCustom, calls=%fused_computation.139 | custom fusion | bytes 12292 | tf_op jit(solution)/shard_map/scatter | solution.py:46
  144.4 16.0 %gather_fusion.1 = bf16[3072,2048]{1,0:T(8,128)(2,1)} fusion(bf16[192,2048]{1,0:T(8,128)(2,1)S(1)} %copy-done, s32[3072]{0:T(1024)S(1)} %fusion.21), kind=kCustom, calls=%fused_computation.3 | custom fusion | bytes 25178112 | tf_op jit(solution)/shard_map/jit(_take)/gather | solution.py:47
  160.4 10.6 %broadcast_select_fusion = bf16[8,8,48,2048]{3,2,1,0:T(8,128)(2,1)} fusion(bf16[8,8,48,2048]{3,2,1,0:T(8,128)(2,1)} %bitcast.171, pred[8,8,48]{2,1,0:T(8,128)(4,1)S(1)} %broadcast_in_dim.105), kind=kLoop, calls=%fused_computation.9 | loop fusion | flops 6291456 | bytes 25168896 | tf_op jit(solution)/shard_map/jit(_take)/select_n | solution.py:47
  171.0 4.3 all-to-all-start.1
  175.6 0.1 convert_reduce_fusion
  176.2 6.9 %gather_fusion.3 = s32[1536]{0:T(1024)S(1)} fusion(s32[8,8]{0,1:T(8,128)S(1)} %bitcast.167, s32[1536]{0:T(1024)S(1)} %reshape.465), kind=kCustom, calls=%fused_computation.5 | custom fusion | bytes 24576 | tf_op jit(solution)/shard_map/jit(take_along_axis)/gather | solution.py:60
  183.2 131.0 %all-to-all-done.1 = bf16[8,8,48,2048]{3,2,1,0:T(8,128)(2,1)} async-done(((bf16[8,8,48,2048]{3,2,1,0:T(8,128)(2,1)}), bf16[8,8,48,2048]{3,2,1,0:T(8,128)(2,1)}, u32[]{:S(2)}, u32[]{:S(2)}) %all-to-all-start.1) | async-done | bytes 12582944 | tf_op jit(solution)/shard_map/all_to_all | solution.py:52
  314.2 18.9 %gather_fusion.4 = bf16[1536,2048]{1,0:T(8,128)(2,1)} fusion(bf16[3072,2048]{1,0:T(8,128)(2,1)} %bitcast.137, s32[2048]{0:T(1024)S(1)} %pad_clamp_fusion.1), kind=kCustom, calls=%fused_computation.clone | custom fusion | bytes 12589056 | tf_op jit(solution)/shard_map/jit(_take)/gather | solution.py:64
  333.1 5.9 %broadcast_select_fusion.2 = bf16[1536,2048]{1,0:T(8,128)(2,1)} fusion(bf16[1536,2048]{1,0:T(8,128)(2,1)} %gather_fusion.4, pred[1536]{0:T(1024)(128)(4,1)S(1)} %get-tuple-element.69), kind=kLoop, calls=%fused_computation.24 | loop fusion | flops 3145728 | bytes 12584448 | tf_op jit(solution)/shard_map/jit(_take)/select_n | solution.py:64
  339.1 28.7 %convolution_convert_fusion = bf16[8,192,2048]{2,1,0:T(8,128)(2,1)} fusion(bf16[8,1024,2048]{2,1,0:T(8,128)(2,1)} %param.11, bf16[8,192,2048]{2,1,0:T(8,128)(2,1)} %bitcast.172, bf16[8,2048,1024]{2,1,0:T(8,128)(2,1)} %param.10), kind=kOutput, calls=%fused_computation.25 | convolution fusion | flops 12902203392 | bytes 79691776 | tf_op jit(solution)/shard_map/ecf,efd->ecd/dot_general | solution.py:68
  367.7 27.4 %gather_fusion.2 = bf16[3072,2048]{1,0:T(8,128)(2,1)} fusion(bf16[1536,2048]{1,0:T(8,128)(2,1)} %bitcast.169, s32[3072]{0:T(1024)S(1)} %broadcast_clamp_fusion), kind=kCustom, calls=%fused_computation.4 | custom fusion | bytes 25178112 | tf_op jit(solution)/shard_map/jit(_take)/gather | solution.py:74
  395.2 10.7 %broadcast_select_fusion.1 = bf16[8,8,48,2048]{3,2,1,0:T(8,128)(2,1)} fusion(bf16[8,8,48,2048]{3,2,1,0:T(8,128)(2,1)} %bitcast.170, pred[8,8,48]{2,1,0:T(8,128)(4,1)S(1)} %compare_and_fusion), kind=kLoop, calls=%fused_computation.10 | loop fusion | flops 6291456 | bytes 25168896 | tf_op jit(solution)/shard_map/jit(_take)/select_n | solution.py:74
  405.9 4.4 all-to-all-start.2
  410.3 0.1 copy.26
  410.5 138.6 %all-to-all-done.2 = bf16[8,8,48,2048]{3,2,1,0:T(8,128)(2,1)} async-done(((bf16[8,8,48,2048]{3,2,1,0:T(8,128)(2,1)}), bf16[8,8,48,2048]{3,2,1,0:T(8,128)(2,1)}, u32[]{:S(2)}, u32[]{:S(2)}) %all-to-all-start.2) | async-done | bytes 12582944 | tf_op jit(solution)/shard_map/all_to_all | solution.py:76
  549.1 19.0 %gather_fusion.5 = bf16[1536,2048]{1,0:T(8,128)(2,1)} fusion(bf16[3072,2048]{1,0:T(8,128)(2,1)} %bitcast.142, s32[2048]{0:T(1024)S(1)} %pad_clamp_fusion), kind=kCustom, calls=%fused_computation.1.clone | custom fusion | bytes 12589056 | tf_op jit(solution)/shard_map/jit(_take)/gather | solution.py:78
  568.0 4.7 fusion.8
  572.7 1.5 fusion.18
  (55 shorter events, 1.6 us)
Async XLA Ops:
  0.0 144.4 %copy-start = (bf16[192,2048]{1,0:T(8,128)(2,1)S(1)}, bf16[192,2048]{1,0:T(8,128)(2,1)}, u32[]{:S(2)}) copy-start(bf16[192,2048]{1,0:T(8,128)(2,1)} %param.7) | copy-start | bytes 2359300
  28.6 142.4 %all-to-all-start = ((s32[8,8,2]{1,2,0:T(2,128)}), s32[8,8,2]{1,2,0:T(2,128)S(1)}, u32[]{:S(2)}, u32[]{:S(2)}) async-start(s32[8,8,2]{1,2,0:T(2,128)} %copy.22), calls=%async_computation | async-start | bytes 16384 | tf_op jit(solution)/shard_map/all_to_all | solution.py:51
  98.1 40.0 %copy-start.1 = (s32[1536]{0:T(1024)}, s32[1536]{0:T(1024)S(1)}, u32[]{:S(2)}) copy-start(s32[1536]{0:T(1024)S(1)} %get-tuple-element.68) | copy-start | bytes 18436
  171.0 143.1 %all-to-all-start.1 = ((bf16[8,8,48,2048]{3,2,1,0:T(8,128)(2,1)}), bf16[8,8,48,2048]{3,2,1,0:T(8,128)(2,1)}, u32[]{:S(2)}, u32[]{:S(2)}) async-start(bf16[8,8,48,2048]{3,2,1,0:T(8,128)(2,1)} %broadcast_select_fusion), calls=%async_computation.1 | async-start | bytes 25165824 | tf_op jit(solution)/shard_map/all_to_all | solution.py:52
  405.9 4.4 copy-start.3
  405.9 4.6 copy-start.2
  405.9 143.2 %all-to-all-start.2 = ((bf16[8,8,48,2048]{3,2,1,0:T(8,128)(2,1)}), bf16[8,8,48,2048]{3,2,1,0:T(8,128)(2,1)}, u32[]{:S(2)}, u32[]{:S(2)}) async-start(bf16[8,8,48,2048]{3,2,1,0:T(8,128)(2,1)} %broadcast_select_fusion.1), calls=%async_computation.2 | async-start | bytes 25165824 | tf_op jit(solution)/shard_map/all_to_all | solution.py:76
  549.1 19.0 %copy-start.4 = (pred[1536]{0:T(1024)(128)(4,1)S(1)}, pred[1536]{0:T(1024)(128)(4,1)}, u32[]{:S(2)}) copy-start(pred[1536]{0:T(1024)(128)(4,1)} %get-tuple-element.67) | copy-start | bytes 4612
where the time goes:
time: 576 us; the launch traced here: 574 us
  waiting for transfers between devices  270 us (47%)
  other arithmetic  127 us (22%)
  local copies, waits for them, and re-layouts  121 us (21%)
  matrix products  33.3 us (6%)
  blocking collectives  11 us (2%)
  starting transfers between devices  10.7 us (2%)
    all_to_all x1, waiting for transfers between devices, device_fn(): returned = lax.all_to_all(back_rows, GRID_AXES, 0, 0, tiled=True)  139 us
    all_to_all x1, waiting for transfers between devices, device_fn(): recv_rows = lax.all_to_all(send_rows, GRID_AXES, 0, 0, tiled=True)  131 us
    select_n x1, other arithmetic, device_fn(): jnp.where(global_rank < capacity, jnp.arange(pair_count, dtype=jnp.int32)...  39.9 us
    sub x1, other arithmetic, local_ranks(): jnp.arange(pair_count, dtype=jnp.int32) - starts[flat_ids[sort_order]]  35.6 us
    dot_general x1, matrix products, device_fn(): jnp.einsum('ecf,efd->ecd', hidden, w_out, preferred_element_type=jnp.floa...  28.7 us
    gather x1, local copies, waits for them, and re-layouts, device_fn(): jnp.take(expert_out.reshape(-1, model_width), back_index.reshape(-1), axi...  27.4 us
    gather x1, local copies, waits for them, and re-layouts, device_fn(): jnp.take(returned.reshape(-1, model_width), send_pos, axis=0, mode='fill'...  19 us
    gather x1, local copies, waits for them, and re-layouts, device_fn(): jnp.take(recv_rows.reshape(-1, model_width), recv_index.reshape(-1), axis...  18.9 us
  transfers between devices with their start and end apart: 3, of which 2 were waited for; matrix products, arithmetic and copies ran while one was open for 26% of the time, Pallas kernels for 0%

commit v1 on v0

v1 whole, which is shorter than its diff:
```python
import functools

import jax
import jax.numpy as jnp
from jax import lax
from jax.experimental import pallas as pl
from jax.experimental.pallas import tpu as pltpu
from jax.sharding import PartitionSpec as P

GRID_AXES = ('row', 'col')
MESH = pl.DeviceIdType.MESH
BF = jnp.bfloat16
F32 = jnp.float32
NI = 12
NO = 12
WIN = 64
DIRECT = (1, 2, 4, 6)
REMOTE = (2, 4, 6)


def moe_kernel(cfg, ids_ref, gate_ref, tok_hbm, wi_hbm, wo_hbm, out_ref,
               ids_all, gate_all, tok_all, pmat, cmat, hacc, hbf, wi, wo, obuf, d2d_in, ici_out, ici_in, own,
               slot_buf, zbuf, start_v, start_s,
               tok_sem, wi_sem, wo_sem, ms_sem, mr_sem, gs_sem, gr_sem, as_sem, ar_sem, ds_sem, dr_sem, is_sem, ir_sem, st_sem):
    tok_dev, cap, nexp, nch, wd, ff = cfg
    ntok = 8 * tok_dev
    i = lax.axis_index('row')
    j = lax.axis_index('col')
    j_flip = j + 1 - 2 * lax.rem(j, 2)

    def rel(r):
        jj = j_flip if r & 1 else j
        if r & 2:
            jj = lax.rem(jj + 2, 4)
        ii = lax.rem(i + 1, 2) if r & 4 else i
        return ii, jj

    def dev(r):
        ii, jj = rel(r)
        return {'row': ii, 'col': jj}

    def gidx(r):
        ii, jj = rel(r)
        return ii * 4 + jj

    def rows_of(r):
        return pl.ds(pl.multiple_of(gidx(r) * tok_dev, 64), tok_dev)

    me = gidx(0)

    def tok_copy(c):
        return pltpu.make_async_copy(tok_hbm.at[:, pl.ds(c * wd, wd)], tok_all.at[c, rows_of(0), :], tok_sem.at[c])

    def wi_copy(s):
        c, e = s // nexp, lax.rem(s, nexp)
        slot = lax.rem(s, NI)
        return pltpu.make_async_copy(wi_hbm.at[e, pl.ds(pl.multiple_of(c * wd, wd), wd), :], wi.at[slot], wi_sem.at[slot])

    def wo_copy(s):
        c, e = s // nexp, lax.rem(s, nexp)
        slot = lax.rem(s, NO)
        return pltpu.make_async_copy(wo_hbm.at[e, :, pl.ds(pl.multiple_of(c * wd, wd), wd)], wo.at[slot], wo_sem.at[slot])

    for c in range(nch):
        tok_copy(c).start()

    def prefetch_i(s, _):
        wi_copy(s).start()
        return 0

    def prefetch_o(s, _):
        wo_copy(s).start()
        return 0

    lax.fori_loop(0, NI, prefetch_i, 0)
    lax.fori_loop(0, NO, prefetch_o, 0)
    ids_all[me] = ids_ref[...]
    gate_all[me] = gate_ref[...]

    bar = pltpu.get_barrier_semaphore()
    for r in range(1, 8):
        pl.semaphore_signal(bar, inc=1, device_id=dev(r), device_id_type=MESH)
    pl.semaphore_wait(bar, 7)

    def ids_copy(r):
        return pltpu.make_async_remote_copy(ids_ref, ids_all.at[me], ms_sem.at[r - 1], mr_sem.at[r - 1],
                                            device_id=dev(r), device_id_type=MESH)

    def gate_copy(r):
        return pltpu.make_async_remote_copy(gate_ref, gate_all.at[me], gs_sem.at[r - 1], gr_sem.at[r - 1],
                                            device_id=dev(r), device_id_type=MESH)

    def ag_copy(c, r, origin, to):
        ref = tok_all.at[c, rows_of(origin), :]
        return pltpu.make_async_remote_copy(ref, ref, as_sem.at[c, r - 1], ar_sem.at[c, r - 1],
                                            device_id=dev(to), device_id_type=MESH)

    for r in range(1, 8):
        ids_copy(r).start()
        gate_copy(r).start()
    for c in range(nch):
        tok_copy(c).wait()
        for r in DIRECT:
            ag_copy(c, r, 0, r).start()

    for r in range(1, 8):
        ids_copy(r).wait_recv()
        gate_copy(r).wait_recv()

    lane = lax.broadcasted_iota(jnp.int32, (8, 128), 1)

    def compact(ref):
        out = []
        for m in range(4):
            a = ref[2 * m]
            b = pltpu.roll(ref[2 * m + 1], 64, 1)
            out += [a[:, :128], jnp.where(lane < 64, a[:, 128:], b[:, :128]), b[:, 128:]]
        return out

    id_blocks, gate_blocks = compact(ids_all), compact(gate_all)
    eid = lax.broadcasted_iota(jnp.int32, (8, 128), 0) + me * nexp
    imasks, gates = [], []
    for idb, gb in zip(id_blocks, gate_blocks):
        m = jnp.zeros((8, 128), jnp.int32)
        g = jnp.zeros((8, 128), F32)
        for k in range(8):
            hit = idb[k:k + 1, :] == eid
            m = jnp.where(hit, 1, m)
            g = jnp.where(hit, gb[k:k + 1, :], g)
        imasks.append(m)
        gates.append(g)
    masks = [m.astype(F32) for m in imasks]
    nb = len(masks)
    tri = jnp.where(lax.broadcasted_iota(jnp.int32, (128, 128), 0) < lax.broadcasted_iota(jnp.int32, (128, 128), 1),
                    1.0, 0.0).astype(BF)
    cums = jnp.dot(jnp.concatenate(masks, axis=0).astype(BF), tri, preferred_element_type=F32)
    carry = jnp.zeros((8, 1), F32)
    ranks = []
    for b in range(nb):
        ranks.append(cums[b * 8:b * 8 + 8, :] + carry)
        carry = carry + jnp.sum(masks[b], axis=1, keepdims=True)
    starts, seen = [], jnp.zeros((8, 128), jnp.int32)
    table = jnp.zeros((8, 128), jnp.int32)
    for g in range(8):
        b = 3 * (g // 2) + g % 2
        before = seen + jnp.where(lane < 64, imasks[b], 0) if g % 2 else seen
        off = jnp.sum(before, axis=1, keepdims=True)
        start16 = jnp.minimum(off >> 4, (cap - WIN) // 16)
        table = jnp.where(lane == g, start16, table)
        starts.append((start16 * 16).astype(F32))
        seen = seen + imasks[b]
        if g % 2:
            seen = seen + imasks[b + 1]
    start_v[...] = table
    st = pltpu.make_async_copy(start_v, start_s, st_sem)
    st.start()
    for b in range(nb):
        m = b // 3
        if b % 3 == 0:
            start = starts[2 * m]
        elif b % 3 == 1:
            start = jnp.where(lane < 64, starts[2 * m], starts[2 * m + 1])
        else:
            start = starts[2 * m + 1]
        keep = (masks[b] > 0.0) & (ranks[b] < float(cap))
        slot_buf[:, b * 128:(b + 1) * 128] = jnp.where(keep, ranks[b], -1.0)
        g1 = gates[b].astype(BF).astype(F32)
        rem1 = gates[b] - g1
        g2 = rem1.astype(BF).astype(F32)
        g3 = rem1 - g2
        zbuf[b, 0:8, :] = jnp.where(keep, ranks[b] - start, -1.0)
        zbuf[b, 8:16, :] = g1
        zbuf[b, 16:24, :] = g2
        zbuf[b, 24:32, :] = g3

    def build_p(e, _):
        row = slot_buf[pl.ds(e, 1), :]
        pos = lax.broadcasted_iota(jnp.int32, (cap, ntok), 0).astype(F32)
        pmat[pl.ds(pl.multiple_of(e * cap, 64), cap), :] = jnp.where(pos == row, 1.0, 0.0).astype(BF)
        return 0

    lax.fori_loop(0, nexp, build_p, 0)
    nwin = nexp * WIN

    def build_c(b, _):
        z = jnp.concatenate([zbuf[b], jnp.zeros((96, 128), F32)], axis=0)
        zt = jnp.transpose(z).astype(BF)
        ex = jnp.where(lax.broadcasted_iota(jnp.int32, (128, 4 * nwin), 0)
                       == lax.broadcasted_iota(jnp.int32, (128, 4 * nwin), 1) // WIN, 1.0, 0.0).astype(BF)
        y = jnp.dot(zt, ex, preferred_element_type=F32)
        wpos = lax.rem(lax.broadcasted_iota(jnp.int32, (128, nwin), 1), WIN).astype(F32)
        hit = y[:, :nwin] == wpos
        rows = pl.ds(pl.multiple_of(b * 128, 128), 128)
        for k in range(3):
            cmat[k, rows, :] = jnp.where(hit, y[:, (k + 1) * nwin:(k + 2) * nwin], 0.0).astype(BF)
        return 0

    lax.fori_loop(0, nb, build_c, 0)

    def first(c, last):
        for r in DIRECT:
            ag_copy(c, r, 0, r).wait_recv()
            if r in REMOTE:
                ag_copy(c, r + 1, r, 1).start()
        for r in REMOTE:
            ag_copy(c, r + 1, 0, 1).wait_recv()

        def pair(q, _):
            for h in range(2):
                e = q * 2 + h
                s = c * nexp + e
                slot = lax.rem(s, NI)
                wi_copy(s).wait()
                bufr = jnp.dot(pmat[pl.ds(pl.multiple_of(e * cap, 64), cap), :], tok_all[c],
                               preferred_element_type=F32).astype(BF)
                for n in range(2):
                    y = jnp.dot(bufr, wi[slot, :, n * (ff // 2):(n + 1) * (ff // 2)], preferred_element_type=F32)
                    if c > 0:
                        y = y + hacc[e * 2 + n]
                    if last:
                        hbf[pl.ds(pl.multiple_of(e * cap, 64), cap), n * (ff // 2):(n + 1) * (ff // 2)] = (
                            jax.nn.gelu(y, approximate=True).astype(BF))
                    else:
                        hacc[e * 2 + n] = y

                @pl.when(s + NI < nch * nexp)
                def _():
                    wi_copy(s + NI).start()
            return 0

        lax.fori_loop(0, nexp // 2, pair, 0)

    for c in range(nch):
        first(c, c == nch - 1)
    st.wait()

    def d2d_copy(c, q):
        k = c * 4 + q
        return pltpu.make_async_remote_copy(hacc.at[k], d2d_in.at[k], ds_sem.at[k], dr_sem.at[k],
                                            device_id=dev(1), device_id_type=MESH)

    def ici_copy(c, q):
        k = c * 3 + q
        return pltpu.make_async_remote_copy(ici_out.at[k], ici_in.at[k], is_sem.at[k], ir_sem.at[k],
                                            device_id=dev(REMOTE[q]), device_id_type=MESH)

    def combine(r):
        g = gidx(r)
        parts = []
        for e in range(nexp):
            at = e * (cap // 16) + start_s[e, g]
            parts.append(obuf[pl.ds(at, WIN // 16)].reshape(WIN, wd))
        win = jnp.concatenate(parts, axis=0)
        rows = pl.ds(pl.multiple_of(g * tok_dev, 64), tok_dev)
        lhs = jnp.concatenate([cmat[k, rows, :] for k in range(3)], axis=0)
        y = jnp.dot(lhs, win, preferred_element_type=F32)
        return y[:tok_dev] + y[tok_dev:2 * tok_dev] + y[2 * tok_dev:]

    def second(c, _):
        def pair(q, _):
            for h in range(2):
                e = q * 2 + h
                s = c * nexp + e
                slot = lax.rem(s, NO)
                wo_copy(s).wait()
                rows = pl.ds(pl.multiple_of(e * cap, 64), cap)
                y = jnp.dot(hbf[rows, :], wo[slot], preferred_element_type=F32).astype(BF)
                obuf[pl.ds(e * (cap // 16), cap // 16)] = y.reshape(cap // 16, 16, wd)

                @pl.when(s + NO < nch * nexp)
                def _():
                    wo_copy(s + NO).start()
            return 0

        lax.fori_loop(0, nexp // 2, pair, 0)
        for q, r in enumerate((2, 4, 6, 0)):
            hacc[c * 4 + q] = combine(r + 1)
            d2d_copy(c, q).start()
        for q, r in enumerate((2, 4, 6, 0)):
            y = combine(r)
            d2d_copy(c, q).wait_recv()
            y = y + d2d_in[c * 4 + q]
            if r:
                ici_out[c * 3 + q] = y.astype(BF)
                ici_copy(c, q).start()
            else:
                own[c] = y
        return 0

    lax.fori_loop(0, nch, second, 0)

    for c in range(nch):
        y = tok_all[c, rows_of(0), :].astype(F32) + own[c]
        for q in range(3):
            ici_copy(c, q).wait_recv()
            y = y + ici_in[c * 3 + q].astype(F32)
        out_ref[:, c * wd:(c + 1) * wd] = y.astype(BF)

    for r in range(1, 8):
        ids_copy(r).wait_send()
        gate_copy(r).wait_send()
    for c in range(nch):
        for r in DIRECT:
            ag_copy(c, r, 0, r).wait_send()
        for r in REMOTE:
            ag_copy(c, r + 1, r, 1).wait_send()
        for q in range(4):
            d2d_copy(c, q).wait_send()
        for q in range(3):
            ici_copy(c, q).wait_send()


def solution(mesh):
    group_size = mesh.shape['row'] * mesh.shape['col']

    def device_fn(tokens, expert_ids, gate_weights, w_in, w_out):
        tok_dev, width = tokens.shape
        top_k = expert_ids.shape[1]
        nexp, _, ff = w_in.shape
        cap = tok_dev * group_size * top_k // (nexp * group_size)
        ntok = tok_dev * group_size
        nch = 4
        wd = width // nch
        ids = jnp.pad(expert_ids.T, ((0, 0), (0, 256 - tok_dev)), constant_values=-1)
        gates = jnp.pad(gate_weights.T, ((0, 0), (0, 256 - tok_dev)))
        dma = pltpu.SemaphoreType.DMA
        cfg = (tok_dev, cap, nexp, nch, wd, ff)
        vm = pl.BlockSpec(memory_space=pltpu.VMEM)
        hb = pl.BlockSpec(memory_space=pl.ANY)
        return pl.pallas_call(
            functools.partial(moe_kernel, cfg),
            out_shape=jax.ShapeDtypeStruct((tok_dev, width), BF),
            in_specs=[vm, vm, hb, hb, hb],
            out_specs=vm,
            scratch_shapes=[
                pltpu.VMEM((8, 8, 256), jnp.int32),
                pltpu.VMEM((8, 8, 256), F32),
                pltpu.VMEM((nch, ntok, wd), BF),
                pltpu.VMEM((nexp * cap, ntok), BF),
                pltpu.VMEM((3, ntok, nexp * WIN), BF),
                pltpu.VMEM((nexp * 2, cap, ff // 2), F32),
                pltpu.VMEM((nexp * cap, ff), BF),
                pltpu.VMEM((NI, wd, ff), BF),
                pltpu.VMEM((NO, ff, wd), BF),
                pltpu.VMEM((nexp * cap // 16, 16, wd), BF),
                pltpu.VMEM((nch * 4, tok_dev, wd), F32),
                pltpu.VMEM((nch * 3, tok_dev, wd), BF),
                pltpu.VMEM((nch * 3, tok_dev, wd), BF),
                pltpu.VMEM((nch, tok_dev, wd), F32),
                pltpu.VMEM((8, ntok), F32),
                pltpu.VMEM((ntok // 128, 32, 128), F32),
                pltpu.VMEM((8, 128), jnp.int32),
                pltpu.SMEM((8, 128), jnp.int32),
                dma((nch,)), dma((NI,)), dma((NO,)), dma((7,)), dma((7,)), dma((7,)), dma((7,)), dma((nch, 7)), dma((nch, 7)),
                dma((nch * 4,)), dma((nch * 4,)), dma((nch * 3,)), dma((nch * 3,)), dma,
            ],
            compiler_params=pltpu.CompilerParams(collective_id=0, has_side_effects=True, vmem_limit_bytes=67000000),
        )(ids, gates, tokens, w_in, w_out)

    token_spec = P(('data', 'row', 'col'), None)
    expert_spec = P(GRID_AXES, None, None)
    return jax.shard_map(device_fn, mesh=mesh, in_specs=(token_spec, token_spec, token_spec, expert_spec, expert_spec),
                         out_specs=token_spec, check_vma=False)
```

time: 576 us -> 101 us (0.18)
  waiting for transfers between devices: 270 us -> 0 us
  other arithmetic: 127 us -> 0 us
  local copies, waits for them, and re-layouts: 121 us -> 4.68 us
  Pallas kernels: 0 us -> 96 us
  matrix products: 33.3 us -> 0 us
  blocking collectives: 11 us -> 0 us
  starting transfers between devices: 10.7 us -> 0 us
    all_to_all x3 -> x0, waiting for transfers between devices: 270 us -> none  [the longest x1 139 us: device_fn(): returned = lax.all_to_all(back_rows, GRID_AXES, 0, 0, tiled=True)]
    gather x15 -> x0, local copies, waits for them, and re-layouts: 102 us -> none  [the longest x1 27.4 us: device_fn(): jnp.take(expert_out.reshape(-1, model_width), back_index.reshape(-1), axi...]
    pallas_call x0 -> x1, Pallas kernels: none -> 96 us  [device_fn(): pl.pallas_call(functools.partial(moe_kernel, cfg), out_shape=jax.ShapeDty...]
    select_n x8 -> x0, other arithmetic: 67.4 us -> none  [the longest x1 39.9 us: device_fn(): jnp.where(global_rank < capacity, jnp.arange(pair_count, dtype=jnp.int32)...]
    sub x2 -> x0, other arithmetic: 35.6 us -> none  [the longest x1 35.6 us: local_ranks(): jnp.arange(pair_count, dtype=jnp.int32) - starts[flat_ids[sort_order]]]
    dot_general x2 -> x0, matrix products: 33.3 us -> none  [the longest x1 28.7 us: device_fn(): jnp.einsum('ecf,efd->ecd', hidden, w_out, preferred_element_type=jnp.floa...]
    scatter x2 -> x0, local copies, waits for them, and re-layouts: 12.4 us -> none  [the longest x1 6.19 us: device_fn(): jnp.full((num_experts * per_source,), tok_dev, jnp.int32).at[send_pos]]
    scatter-add x1 -> x0, other arithmetic: 11.1 us -> none  [local_ranks(): counts = jnp.zeros((num_experts,), jnp.int32).at[flat_ids].add(1)]
  transfers between devices with their start and end apart: 3 -> 0, of which waited for: 2 -> 0; matrix products, arithmetic and copies ran while one was open for 26% -> 0% of each run, Pallas kernels for 0% -> 0%
where the time goes in v1:
time: 101 us
  Pallas kernels  96 us (95%)
  local copies, waits for them, and re-layouts  4.68 us (5%)
    pallas_call x1, Pallas kernels, device_fn(): pl.pallas_call(functools.partial(moe_kernel, cfg), out_shape=jax.ShapeDty...  96 us
    unnamed x1, local copies, waits for them, and re-layouts  2.09 us

profile of v1, /device:TPU:0, one launch (start us, length us, event | category | flops | bytes accessed | tf_op | source)
XLA Modules:
  0.0 100.7 jit_solution(7928442460505851774)
XLA Ops:
  0.0 1.3 %pad.8.ids_ref = s32[8,256]{1,0:T(8,128)} pad(s32[8,192]{1,0:T(8,128)} %bitcast.2, s32[]{:T(128)} %constant.1.clone.1), padding=0_0x0_64 | pad | bytes 14340 | tf_op jit(solution)/shard_map/jit(_pad)/pad | solution.py:324
  1.3 1.3 %pad.9.gate_ref = f32[8,256]{1,0:T(8,128)} pad(f32[8,192]{1,0:T(8,128)} %bitcast.3, f32[]{:T(128)} %constant.4.clone.1), padding=0_0x0_64 | pad | bytes 14340 | tf_op jit(solution)/shard_map/jit(_pad)/pad | solution.py:325
  2.6 96.0 %shard_map.55 = bf16[192,2048]{1,0:T(8,128)(2,1)} custom-call(s32[8,256]{1,0:T(8,128)} %pad.8.ids_ref, f32[8,256]{1,0:T(8,128)} %pad.9.gate_ref, bf16[192,2048]{1,0:T(8,128)(2,1)} %tok_hbm.1, bf16[8,2048,1024]{2,1,0:T(8,128)(2,1)} %wi_hbm.1, bf16[8,1024,2048]{2,1,0:T(8,128)(2,1)} %wo_hbm.1), custom_call_target="tpu_custom_call" | custom-call | tf_op jit(solution)/shard_map/pallas_call | solution.py:330
  98.6 2.1 %copy.7 = bf16[192,2048]{1,0:T(8,128)(2,1)} copy(bf16[192,2048]{1,0:T(8,128)(2,1)} %shard_map.55) | data formatting | bytes 1572864

commit v2 on v1

--- a/solution.py
+++ b/solution.py
@@ -11,19 +11,22 @@
 MESH = pl.DeviceIdType.MESH
 BF = jnp.bfloat16
 F32 = jnp.float32
-NI = 12
-NO = 12
+NI = 20
+NO = 20
 WIN = 64
-DIRECT = (1, 2, 4, 6)
-REMOTE = (2, 4, 6)
-
-
-def moe_kernel(cfg, ids_ref, gate_ref, tok_hbm, wi_hbm, wo_hbm, out_ref,
-               ids_all, gate_all, tok_all, pmat, cmat, hacc, hbf, wi, wo, obuf, d2d_in, ici_out, ici_in, own,
+LEAD = 2
+AG_KINDS = ((0, None, 1), (0, None, 2), (0, None, 4), (2, 0, 4), (4, 1, 2), (2, None, 1), (4, None, 1), (6, 0, 1), (6, 1, 1))
+RETURN_ORDER = (6, 2, 4, 0)
+
+
+def moe_kernel(cfg, ids_ref, gate_ref, tok_hbm, wi_hbm, wo_hbm, out_hbm,
+               ids_all, gate_all, tok_all, pmat, cmat, hacc, hbf, wi, wo, obuf, d2d_in, out1, in1, out2, in2, kept, own, outv,
                slot_buf, zbuf, start_v, start_s,
-               tok_sem, wi_sem, wo_sem, ms_sem, mr_sem, gs_sem, gr_sem, as_sem, ar_sem, ds_sem, dr_sem, is_sem, ir_sem, st_sem):
+               tok_sem, wi_sem, wo_sem, ms_sem, mr_sem, gs_sem, gr_sem, as_sem, ar_sem, ds_sem, dr_sem,
+               s1_sem, r1_sem, s2_sem, r2_sem, st_sem, out_sem):
     tok_dev, cap, nexp, nch, wd, ff = cfg
     ntok = 8 * tok_dev
+    half = tok_dev // 2
     i = lax.axis_index('row')
     j = lax.axis_index('col')
     j_flip = j + 1 - 2 * lax.rem(j, 2)
@@ -61,6 +64,9 @@
         slot = lax.rem(s, NO)
         return pltpu.make_async_copy(wo_hbm.at[e, :, pl.ds(pl.multiple_of(c * wd, wd), wd)], wo.at[slot], wo_sem.at[slot])
 
+    def out_copy(c):
+        return pltpu.make_async_copy(outv.at[c], out_hbm.at[:, pl.ds(pl.multiple_of(c * wd, wd), wd)], out_sem.at[c])
+
     for c in range(nch):
         tok_copy(c).start()
 
@@ -74,8 +80,10 @@
 
     lax.fori_loop(0, NI, prefetch_i, 0)
     lax.fori_loop(0, NO, prefetch_o, 0)
-    ids_all[me] = ids_ref[...]
-    gate_all[me] = gate_ref[...]
+    ids_all[me] = jnp.zeros((8, 256), jnp.int32)
+    ids_all[me, :, :tok_dev] = ids_ref[...]
+    gate_all[me] = jnp.zeros((8, 256), F32)
+    gate_all[me, :, :tok_dev] = gate_ref[...]
 
     bar = pltpu.get_barrier_semaphore()
     for r in range(1, 8):
@@ -83,25 +91,48 @@
     pl.semaphore_wait(bar, 7)
 
     def ids_copy(r):
-        return pltpu.make_async_remote_copy(ids_ref, ids_all.at[me], ms_sem.at[r - 1], mr_sem.at[r - 1],
+        return pltpu.make_async_remote_copy(ids_all.at[me], ids_all.at[me], ms_sem.at[r - 1], mr_sem.at[r - 1],
                                             device_id=dev(r), device_id_type=MESH)
 
     def gate_copy(r):
-        return pltpu.make_async_remote_copy(gate_ref, gate_all.at[me], gs_sem.at[r - 1], gr_sem.at[r - 1],
+        return pltpu.make_async_remote_copy(gate_all.at[me], gate_all.at[me], gs_sem.at[r - 1], gr_sem.at[r - 1],
                                             device_id=dev(r), device_id_type=MESH)
 
-    def ag_copy(c, r, origin, to):
-        ref = tok_all.at[c, rows_of(origin), :]
-        return pltpu.make_async_remote_copy(ref, ref, as_sem.at[c, r - 1], ar_sem.at[c, r - 1],
+    def ag_copy(c, kind, mine):
+        owner, part, to = AG_KINDS[kind]
+        if not mine:
+            owner = owner ^ to
+        start, size = gidx(owner) * tok_dev, tok_dev
+        if part is not None:
+            start, size = start + part * half, half
+        ref = tok_all.at[c, pl.ds(pl.multiple_of(start, 32), size), :]
+        return pltpu.make_async_remote_copy(ref, ref, as_sem.at[c, kind], ar_sem.at[c, kind],
                                             device_id=dev(to), device_id_type=MESH)
+
+    def send_own(c):
+        tok_copy(c).wait()
+        for kind in (1, 2, 0):
+            ag_copy(c, kind, True).start()
+
+    def near(c):
+        ag_copy(c, 1, False).wait_recv()
+        ag_copy(c, 3, True).start()
+        ag_copy(c, 5, True).start()
+        ag_copy(c, 2, False).wait_recv()
+        ag_copy(c, 4, True).start()
+        ag_copy(c, 6, True).start()
+
+    def far(c):
+        ag_copy(c, 3, False).wait_recv()
+        ag_copy(c, 7, True).start()
+        ag_copy(c, 4, False).wait_recv()
+        ag_copy(c, 8, True).start()
 
     for r in range(1, 8):
         ids_copy(r).start()
         gate_copy(r).start()
-    for c in range(nch):
-        tok_copy(c).wait()
-        for r in DIRECT:
-            ag_copy(c, r, 0, r).start()
+    for c in range(LEAD):
+        send_own(c)
 
     for r in range(1, 8):
         ids_copy(r).wait_recv()
@@ -179,7 +210,6 @@
         pmat[pl.ds(pl.multiple_of(e * cap, 64), cap), :] = jnp.where(pos == row, 1.0, 0.0).astype(BF)
         return 0
 
-    lax.fori_loop(0, nexp, build_p, 0)
     nwin = nexp * WIN
 
     def build_c(b, _):
@@ -195,33 +225,29 @@
             cmat[k, rows, :] = jnp.where(hit, y[:, (k + 1) * nwin:(k + 2) * nwin], 0.0).astype(BF)
         return 0
 
-    lax.fori_loop(0, nb, build_c, 0)
+    def zero(k, _):
+        hacc[k] = jnp.zeros((cap, wd), F32)
+        return 0
 
     def first(c, last):
-        for r in DIRECT:
-            ag_copy(c, r, 0, r).wait_recv()
-            if r in REMOTE:
-                ag_copy(c, r + 1, r, 1).start()
-        for r in REMOTE:
-            ag_copy(c, r + 1, 0, 1).wait_recv()
+        for kind in (0, 5, 6, 7, 8):
+            ag_copy(c, kind, False).wait_recv()
 
         def pair(q, _):
             for h in range(2):
                 e = q * 2 + h
                 s = c * nexp + e
                 slot = lax.rem(s, NI)
+                rows = pl.ds(pl.multiple_of(e * cap, 64), cap)
                 wi_copy(s).wait()
-                bufr = jnp.dot(pmat[pl.ds(pl.multiple_of(e * cap, 64), cap), :], tok_all[c],
-                               preferred_element_type=F32).astype(BF)
-                for n in range(2):
-                    y = jnp.dot(bufr, wi[slot, :, n * (ff // 2):(n + 1) * (ff // 2)], preferred_element_type=F32)
-                    if c > 0:
-                        y = y + hacc[e * 2 + n]
+                bufr = jnp.dot(pmat[rows, :], tok_all[c], preferred_element_type=F32).astype(BF)
+                y = jnp.dot(bufr, wi[slot], preferred_element_type=F32)
+                for n in range(ff // wd):
+                    yn = y[:, n * wd:(n + 1) * wd] + hacc[e * (ff // wd) + n]
                     if last:
-                        hbf[pl.ds(pl.multiple_of(e * cap, 64), cap), n * (ff // 2):(n + 1) * (ff // 2)] = (
-                            jax.nn.gelu(y, approximate=True).astype(BF))
+                        hbf[rows, n * wd:(n + 1) * wd] = jax.nn.gelu(yn, approximate=True).astype(BF)
                     else:
-                        hacc[e * 2 + n] = y
+                        hacc[e * (ff // wd) + n] = yn
 
                 @pl.when(s + NI < nch * nexp)
                 def _():
@@ -230,8 +256,29 @@
 
         lax.fori_loop(0, nexp // 2, pair, 0)
 
-    for c in range(nch):
-        first(c, c == nch - 1)
+    near(0)
+    send_own(LEAD)
+    lax.fori_loop(0, nexp, build_p, 0)
+    lax.fori_loop(0, nexp * ff // wd, zero, 0)
+    near(1)
+    send_own(LEAD + 1)
+    lax.fori_loop(0, nb, build_c, 0)
+    far(0)
+
+    def step(c, _):
+        @pl.when(c < nch)
+        def _():
+            near(c)
+
+        @pl.when(c + LEAD < nch)
+        def _():
+            send_own(c + LEAD)
+        first(c - 2, False)
+        far(c - 1)
+        return 0
+
+    lax.fori_loop(2, nch + 1, step, 0)
+    first(nch - 1, True)
     st.wait()
 
     def d2d_copy(c, q):
@@ -239,10 +286,13 @@
         return pltpu.make_async_remote_copy(hacc.at[k], d2d_in.at[k], ds_sem.at[k], dr_sem.at[k],
                                             device_id=dev(1), device_id_type=MESH)
 
-    def ici_copy(c, q):
-        k = c * 3 + q
-        return pltpu.make_async_remote_copy(ici_out.at[k], ici_in.at[k], is_sem.at[k], ir_sem.at[k],
-                                            device_id=dev(REMOTE[q]), device_id_type=MESH)
+    def hop1(c, axis):
+        return pltpu.make_async_remote_copy(out1.at[c, axis], in1.at[c, axis], s1_sem.at[c, axis], r1_sem.at[c, axis],
+                                            device_id=dev(4 if axis else 2), device_id_type=MESH)
+
+    def hop2(c, part):
+        return pltpu.make_async_remote_copy(out2.at[c, part], in2.at[c, part], s2_sem.at[c, part], r2_sem.at[c, part],
+                                            device_id=dev(2 if part else 4), device_id_type=MESH)
 
     def combine(r):
         g = gidx(r)
@@ -256,6 +306,21 @@
         y = jnp.dot(lhs, win, preferred_element_type=F32)
         return y[:tok_dev] + y[tok_dev:2 * tok_dev] + y[2 * tok_dev:]
 
+    def relay(c):
+        for part in range(2):
+            hop1(c, part).wait_recv()
+            out2[c, part] = (kept[c, part] + in1[c, part, 1].astype(F32)).astype(BF)
+            hop2(c, part).start()
+
+    def finish(c):
+        for part in range(2):
+            hop2(c, part).wait_recv()
+            at = pl.multiple_of(me * tok_dev + part * half, 32)
+            y = tok_all[c, pl.ds(at, half), :].astype(F32) + (
+                own[c, part] + in1[c, part, 0].astype(F32) + in2[c, part].astype(F32))
+            outv[c, part * half:(part + 1) * half, :] = y.astype(BF)
+        out_copy(c).start()
+
     def second(c, _):
         def pair(q, _):
             for h in range(2):
@@ -273,41 +338,58 @@
             return 0
 
         lax.fori_loop(0, nexp // 2, pair, 0)
-        for q, r in enumerate((2, 4, 6, 0)):
+        for q, r in enumerate(RETURN_ORDER):
             hacc[c * 4 + q] = combine(r + 1)
             d2d_copy(c, q).start()
-        for q, r in enumerate((2, 4, 6, 0)):
+        for q, r in enumerate(RETURN_ORDER):
             y = combine(r)
             d2d_copy(c, q).wait_recv()
             y = y + d2d_in[c * 4 + q]
-            if r:
-                ici_out[c * 3 + q] = y.astype(BF)
-                ici_copy(c, q).start()
+            if r == 6:
+                out1[c, 0, 1] = y[:half].astype(BF)
+                out1[c, 1, 1] = y[half:].astype(BF)
+            elif r == 2:
+                out1[c, 0, 0] = y[:half].astype(BF)
+                kept[c, 1] = y[half:]
+                hop1(c, 0).start()
+            elif r == 4:
+                out1[c, 1, 0] = y[half:].astype(BF)
+                kept[c, 0] = y[:half]
+                hop1(c, 1).start()
             else:
-                own[c] = y
+                own[c, 0] = y[:half]
+                own[c, 1] = y[half:]
+
+        @pl.when(c > 0)
+        def _():
+            relay(c - 1)
+
+        @pl.when(c > 1)
+        def _():
+            finish(c - 2)
         return 0
 
     lax.fori_loop(0, nch, second, 0)
-
-    for c in range(nch):
-        y = tok_all[c, rows_of(0), :].astype(F32) + own[c]
-        for q in range(3):
-            ici_copy(c, q).wait_recv()
-            y = y + ici_in[c * 3 + q].astype(F32)
-        out_ref[:, c * wd:(c + 1) * wd] = y.astype(BF)
+    relay(nch - 1)
+    finish(nch - 2)
+    finish(nch - 1)
 
     for r in range(1, 8):
         ids_copy(r).wait_send()
         gate_copy(r).wait_send()
-    for c in range(nch):
-        for r in DIRECT:
-            ag_copy(c, r, 0, r).wait_send()
-        for r in REMOTE:
-            ag_copy(c, r + 1, r, 1).wait_send()
+
+    def drain(c, _):
+        for kind in range(9):
+            ag_copy(c, kind, True).wait_send()
         for q in range(4):
             d2d_copy(c, q).wait_send()
-        for q in range(3):
-            ici_copy(c, q).wait_send()
+        for part in range(2):
+            hop1(c, part).wait_send()
+            hop2(c, part).wait_send()
+        out_copy(c).wait()
+        return 0
+
+    lax.fori_loop(0, nch, drain, 0)
 
 
 def solution(mesh):
@@ -319,10 +401,9 @@
         nexp, _, ff = w_in.shape
         cap = tok_dev * group_size * top_k // (nexp * group_size)
         ntok = tok_dev * group_size
-        nch = 4
+        nch = 8
         wd = width // nch
-        ids = jnp.pad(expert_ids.T, ((0, 0), (0, 256 - tok_dev)), constant_values=-1)
-        gates = jnp.pad(gate_weights.T, ((0, 0), (0, 256 - tok_dev)))
+        half = tok_dev // 2
         dma = pltpu.SemaphoreType.DMA
         cfg = (tok_dev, cap, nexp, nch, wd, ff)
         vm = pl.BlockSpec(memory_space=pltpu.VMEM)
@@ -331,31 +412,35 @@
             functools.partial(moe_kernel, cfg),
             out_shape=jax.ShapeDtypeStruct((tok_dev, width), BF),
             in_specs=[vm, vm, hb, hb, hb],
-            out_specs=vm,
+            out_specs=hb,
             scratch_shapes=[
                 pltpu.VMEM((8, 8, 256), jnp.int32),
                 pltpu.VMEM((8, 8, 256), F32),
                 pltpu.VMEM((nch, ntok, wd), BF),
                 pltpu.VMEM((nexp * cap, ntok), BF),
                 pltpu.VMEM((3, ntok, nexp * WIN), BF),
-                pltpu.VMEM((nexp * 2, cap, ff // 2), F32),
+                pltpu.VMEM((nexp * ff // wd, cap, wd), F32),
                 pltpu.VMEM((nexp * cap, ff), BF),
                 pltpu.VMEM((NI, wd, ff), BF),
                 pltpu.VMEM((NO, ff, wd), BF),
                 pltpu.VMEM((nexp * cap // 16, 16, wd), BF),
                 pltpu.VMEM((nch * 4, tok_dev, wd), F32),
-                pltpu.VMEM((nch * 3, tok_dev, wd), BF),
-                pltpu.VMEM((nch * 3, tok_dev, wd), BF),
-                pltpu.VMEM((nch, tok_dev, wd), F32),
+                pltpu.VMEM((nch, 2, 2, half, wd), BF),
+                pltpu.VMEM((nch, 2, 2, half, wd), BF),
+                pltpu.VMEM((nch, 2, half, wd), BF),
+                pltpu.VMEM((nch, 2, half, wd), BF),
+                pltpu.VMEM((nch, 2, half, wd), F32),
+                pltpu.VMEM((nch, 2, half, wd), F32),
+                pltpu.VMEM((nch, tok_dev, wd), BF),
                 pltpu.VMEM((8, ntok), F32),
                 pltpu.VMEM((ntok // 128, 32, 128), F32),
                 pltpu.VMEM((8, 128), jnp.int32),
                 pltpu.SMEM((8, 128), jnp.int32),
-                dma((nch,)), dma((NI,)), dma((NO,)), dma((7,)), dma((7,)), dma((7,)), dma((7,)), dma((nch, 7)), dma((nch, 7)),
-                dma((nch * 4,)), dma((nch * 4,)), dma((nch * 3,)), dma((nch * 3,)), dma,
+                dma((nch,)), dma((NI,)), dma((NO,)), dma((7,)), dma((7,)), dma((7,)), dma((7,)), dma((nch, 9)), dma((nch, 9)),
+                dma((nch * 4,)), dma((nch * 4,)), dma((nch, 2)), dma((nch, 2)), dma((nch, 2)), dma((nch, 2)), dma, dma((nch,)),
             ],
             compiler_params=pltpu.CompilerParams(collective_id=0, has_side_effects=True, vmem_limit_bytes=67000000),
-        )(ids, gates, tokens, w_in, w_out)
+        )(expert_ids.T, gate_weights.T, tokens, w_in, w_out)
 
     token_spec = P(('data', 'row', 'col'), None)
     expert_spec = P(GRID_AXES, None, None)

time: 101 us -> 138 us (1.37)
  Pallas kernels: 96 us -> 136 us
  local copies, waits for them, and re-layouts: 4.68 us -> 2.09 us
    pallas_call x1, Pallas kernels: 96 us -> 136 us  [device_fn(): pl.pallas_call(functools.partial(moe_kernel, cfg), out_shape=jax.ShapeDty...]
    pad x2 -> x0, local copies, waits for them, and re-layouts: 2.59 us -> none  [the longest x1 1.3 us: device_fn(): jnp.pad(expert_ids.T, ((0, 0), (0, 256 - tok_dev)), constant_values=-1)]
where the time goes in v2:
time: 138 us
  Pallas kernels  136 us (99%)
  local copies, waits for them, and re-layouts  2.09 us (2%)
    pallas_call x1, Pallas kernels, device_fn(): pl.pallas_call(functools.partial(moe_kernel, cfg), out_shape=jax.ShapeDty...  136 us

profile of v2, /device:TPU:0, one launch (start us, length us, event | category | flops | bytes accessed | tf_op | source)
XLA Modules:
  0.0 138.2 jit_solution(17767997449084947956)
XLA Ops:
  0.0 136.1 %shard_map.55 = bf16[192,2048]{1,0:T(8,128)(2,1)} custom-call(s32[8,192]{1,0:T(8,128)} %bitcast.2, f32[8,192]{1,0:T(8,128)} %bitcast.3, bf16[192,2048]{1,0:T(8,128)(2,1)} %tok_hbm.1, bf16[8,2048,1024]{2,1,0:T(8,128)(2,1)} %wi_hbm.1, bf16[8,1024,2048]{2,1,0:T(8,128)(2,1)} %wo_hbm.1), custom_call_target="tpu_custom_call" | custom-call | tf_op jit(solution)/shard_map/pallas_call | solution.py:411
  136.1 2.1 %copy.7 = bf16[192,2048]{1,0:T(8,128)(2,1)} copy(bf16[192,2048]{1,0:T(8,128)(2,1)} %shard_map.55) | data formatting | bytes 1572864

commit v3 on v2

--- a/solution.py
+++ b/solution.py
@@ -11,8 +11,8 @@
 MESH = pl.DeviceIdType.MESH
 BF = jnp.bfloat16
 F32 = jnp.float32
-NI = 20
-NO = 20
+NI = 10
+NO = 10
 WIN = 64
 LEAD = 2
 AG_KINDS = ((0, None, 1), (0, None, 2), (0, None, 4), (2, 0, 4), (4, 1, 2), (2, None, 1), (4, None, 1), (6, 0, 1), (6, 1, 1))
@@ -261,7 +261,8 @@
     lax.fori_loop(0, nexp, build_p, 0)
     lax.fori_loop(0, nexp * ff // wd, zero, 0)
     near(1)
-    send_own(LEAD + 1)
+    if LEAD + 1 < nch:
+        send_own(LEAD + 1)
     lax.fori_loop(0, nb, build_c, 0)
     far(0)
 
@@ -286,9 +287,9 @@
         return pltpu.make_async_remote_copy(hacc.at[k], d2d_in.at[k], ds_sem.at[k], dr_sem.at[k],
                                             device_id=dev(1), device_id_type=MESH)
 
-    def hop1(c, axis):
-        return pltpu.make_async_remote_copy(out1.at[c, axis], in1.at[c, axis], s1_sem.at[c, axis], r1_sem.at[c, axis],
-                                            device_id=dev(4 if axis else 2), device_id_type=MESH)
+    def hop1(c, axis, k):
+        return pltpu.make_async_remote_copy(out1.at[c, axis, k], in1.at[c, axis, k], s1_sem.at[c, axis * 2 + k],
+                                            r1_sem.at[c, axis * 2 + k], device_id=dev(4 if axis else 2), device_id_type=MESH)
 
     def hop2(c, part):
         return pltpu.make_async_remote_copy(out2.at[c, part], in2.at[c, part], s2_sem.at[c, part], r2_sem.at[c, part],
@@ -308,12 +309,13 @@
 
     def relay(c):
         for part in range(2):
-            hop1(c, part).wait_recv()
+            hop1(c, part, 1).wait_recv()
             out2[c, part] = (kept[c, part] + in1[c, part, 1].astype(F32)).astype(BF)
             hop2(c, part).start()
 
     def finish(c):
         for part in range(2):
+            hop1(c, part, 0).wait_recv()
             hop2(c, part).wait_recv()
             at = pl.multiple_of(me * tok_dev + part * half, 32)
             y = tok_all[c, pl.ds(at, half), :].astype(F32) + (
@@ -348,14 +350,16 @@
             if r == 6:
                 out1[c, 0, 1] = y[:half].astype(BF)
                 out1[c, 1, 1] = y[half:].astype(BF)
+                hop1(c, 0, 1).start()
+                hop1(c, 1, 1).start()
             elif r == 2:
                 out1[c, 0, 0] = y[:half].astype(BF)
                 kept[c, 1] = y[half:]
-                hop1(c, 0).start()
+                hop1(c, 0, 0).start()
             elif r == 4:
                 out1[c, 1, 0] = y[half:].astype(BF)
                 kept[c, 0] = y[:half]
-                hop1(c, 1).start()
+                hop1(c, 1, 0).start()
             else:
                 own[c, 0] = y[:half]
                 own[c, 1] = y[half:]
@@ -384,7 +388,8 @@
         for q in range(4):
             d2d_copy(c, q).wait_send()
         for part in range(2):
-            hop1(c, part).wait_send()
+            hop1(c, part, 0).wait_send()
+            hop1(c, part, 1).wait_send()
             hop2(c, part).wait_send()
         out_copy(c).wait()
         return 0
@@ -401,7 +406,7 @@
         nexp, _, ff = w_in.shape
         cap = tok_dev * group_size * top_k // (nexp * group_size)
         ntok = tok_dev * group_size
-        nch = 8
+        nch = 4
         wd = width // nch
         half = tok_dev // 2
         dma = pltpu.SemaphoreType.DMA
@@ -437,7 +442,7 @@
                 pltpu.VMEM((8, 128), jnp.int32),
                 pltpu.SMEM((8, 128), jnp.int32),
                 dma((nch,)), dma((NI,)), dma((NO,)), dma((7,)), dma((7,)), dma((7,)), dma((7,)), dma((nch, 9)), dma((nch, 9)),
-                dma((nch * 4,)), dma((nch * 4,)), dma((nch, 2)), dma((nch, 2)), dma((nch, 2)), dma((nch, 2)), dma, dma((nch,)),
+                dma((nch * 4,)), dma((nch * 4,)), dma((nch, 4)), dma((nch, 4)), dma((nch, 2)), dma((nch, 2)), dma, dma((nch,)),
             ],
             compiler_params=pltpu.CompilerParams(collective_id=0, has_side_effects=True, vmem_limit_bytes=67000000),
         )(expert_ids.T, gate_weights.T, tokens, w_in, w_out)

time: 138 us -> 95.7 us (0.69)
  Pallas kernels: 136 us -> 93.4 us
    pallas_call x1, Pallas kernels: 136 us -> 93.4 us  [device_fn(): pl.pallas_call(functools.partial(moe_kernel, cfg), out_shape=jax.ShapeDty...]
where the time goes in v3:
time: 95.7 us; the launch traced here: 95.5 us
  Pallas kernels  93.4 us (98%)
  local copies, waits for them, and re-layouts  2.09 us (2%)
    pallas_call x1, Pallas kernels, device_fn(): pl.pallas_call(functools.partial(moe_kernel, cfg), out_shape=jax.ShapeDty...  93.4 us
    unnamed x1, local copies, waits for them, and re-layouts  2.09 us

profile of v3, /device:TPU:0, one launch (start us, length us, event | category | flops | bytes accessed | tf_op | source)
XLA Modules:
  0.0 95.5 jit_solution(5444065240527201822)
XLA Ops:
  0.0 93.4 %shard_map.55 = bf16[192,2048]{1,0:T(8,128)(2,1)} custom-call(s32[8,192]{1,0:T(8,128)} %bitcast.2, f32[8,192]{1,0:T(8,128)} %bitcast.3, bf16[192,2048]{1,0:T(8,128)(2,1)} %tok_hbm.1, bf16[8,2048,1024]{2,1,0:T(8,128)(2,1)} %wi_hbm.1, bf16[8,1024,2048]{2,1,0:T(8,128)(2,1)} %wo_hbm.1), custom_call_target="tpu_custom_call" | custom-call | tf_op jit(solution)/shard_map/pallas_call | solution.py:416
  93.4 2.1 %copy.7 = bf16[192,2048]{1,0:T(8,128)(2,1)} copy(bf16[192,2048]{1,0:T(8,128)(2,1)} %shard_map.55) | data formatting | bytes 1572864

commit v4 on v3

--- a/solution.py
+++ b/solution.py
@@ -20,7 +20,7 @@
 
 
 def moe_kernel(cfg, ids_ref, gate_ref, tok_hbm, wi_hbm, wo_hbm, out_hbm,
-               ids_all, gate_all, tok_all, pmat, cmat, hacc, hbf, wi, wo, obuf, d2d_in, out1, in1, out2, in2, kept, own, outv,
+               ids_all, gate_all, tok_all, pmat, cmat, hacc, hbf, wi, wo, obuf, d2d_in, out1, in1, out2, in2, kept, own, mine, outv,
                slot_buf, zbuf, start_v, start_s,
                tok_sem, wi_sem, wo_sem, ms_sem, mr_sem, gs_sem, gr_sem, as_sem, ar_sem, ds_sem, dr_sem,
                s1_sem, r1_sem, s2_sem, r2_sem, st_sem, out_sem):
@@ -225,61 +225,65 @@
             cmat[k, rows, :] = jnp.where(hit, y[:, (k + 1) * nwin:(k + 2) * nwin], 0.0).astype(BF)
         return 0
 
-    def zero(k, _):
-        hacc[k] = jnp.zeros((cap, wd), F32)
-        return 0
-
-    def first(c, last):
+    def arrived(c):
         for kind in (0, 5, 6, 7, 8):
             ag_copy(c, kind, False).wait_recv()
 
-        def pair(q, _):
-            for h in range(2):
-                e = q * 2 + h
-                s = c * nexp + e
-                slot = lax.rem(s, NI)
-                rows = pl.ds(pl.multiple_of(e * cap, 64), cap)
-                wi_copy(s).wait()
-                bufr = jnp.dot(pmat[rows, :], tok_all[c], preferred_element_type=F32).astype(BF)
-                y = jnp.dot(bufr, wi[slot], preferred_element_type=F32)
-                for n in range(ff // wd):
-                    yn = y[:, n * wd:(n + 1) * wd] + hacc[e * (ff // wd) + n]
-                    if last:
-                        hbf[rows, n * wd:(n + 1) * wd] = jax.nn.gelu(yn, approximate=True).astype(BF)
-                    else:
-                        hacc[e * (ff // wd) + n] = yn
-
-                @pl.when(s + NI < nch * nexp)
-                def _():
-                    wi_copy(s + NI).start()
-            return 0
-
-        lax.fori_loop(0, nexp // 2, pair, 0)
-
+    def first(c, part):
+        experts = range(part * (nexp // 2), (part + 1) * (nexp // 2))
+        for e in experts:
+            wi_copy(c * nexp + e).wait()
+
+        def dispatch(e):
+            return jnp.dot(pmat[e * cap:(e + 1) * cap, :], tok_all[c], preferred_element_type=F32).astype(BF)
+
+        def expand(e, rows):
+            y = jnp.dot(rows, wi[(c * nexp + e) % NI], preferred_element_type=F32)
+            for n in range(ff // wd):
+                yn = y[:, n * wd:(n + 1) * wd]
+                if c:
+                    yn = yn + hacc[e * (ff // wd) + n]
+                if c == nch - 1:
+                    hbf[e * cap:(e + 1) * cap, n * wd:(n + 1) * wd] = jax.nn.gelu(yn, approximate=True).astype(BF)
+                else:
+                    hacc[e * (ff // wd) + n] = yn
+
+        ready = None
+        for e in experts:
+            rows = dispatch(e)
+            if ready is not None:
+                expand(*ready)
+            ready = (e, rows)
+        expand(*ready)
+        for e in experts:
+            s = c * nexp + e
+            if s + NI < nch * nexp:
+                wi_copy(s + NI).start()
+
+    lax.fori_loop(0, nexp, build_p, 0)
+    lax.fori_loop(0, nb, build_c, 0)
     near(0)
-    send_own(LEAD)
-    lax.fori_loop(0, nexp, build_p, 0)
-    lax.fori_loop(0, nexp * ff // wd, zero, 0)
+    send_own(2)
     near(1)
-    if LEAD + 1 < nch:
-        send_own(LEAD + 1)
-    lax.fori_loop(0, nb, build_c, 0)
+    send_own(3)
     far(0)
-
-    def step(c, _):
-        @pl.when(c < nch)
-        def _():
-            near(c)
-
-        @pl.when(c + LEAD < nch)
-        def _():
-            send_own(c + LEAD)
-        first(c - 2, False)
-        far(c - 1)
-        return 0
-
-    lax.fori_loop(2, nch + 1, step, 0)
-    first(nch - 1, True)
+    arrived(0)
+    first(0, 0)
+    first(0, 1)
+    near(2)
+    far(1)
+    arrived(1)
+    first(1, 0)
+    near(3)
+    first(1, 1)
+    far(2)
+    arrived(2)
+    first(2, 0)
+    far(3)
+    first(2, 1)
+    arrived(3)
+    first(3, 0)
+    first(3, 1)
     st.wait()
 
     def d2d_copy(c, q):
@@ -324,29 +328,30 @@
         out_copy(c).start()
 
     def second(c, _):
-        def pair(q, _):
-            for h in range(2):
-                e = q * 2 + h
+        for part in range(2):
+            experts = range(part * (nexp // 2), (part + 1) * (nexp // 2))
+            for e in experts:
+                wo_copy(c * nexp + e).wait()
+            for e in experts:
+                slot = lax.rem(c * nexp + e, NO)
+                y = jnp.dot(hbf[e * cap:(e + 1) * cap, :], wo[slot], preferred_element_type=F32).astype(BF)
+                obuf[e * (cap // 16):(e + 1) * (cap // 16)] = y.reshape(cap // 16, 16, wd)
+            for e in experts:
                 s = c * nexp + e
-                slot = lax.rem(s, NO)
-                wo_copy(s).wait()
-                rows = pl.ds(pl.multiple_of(e * cap, 64), cap)
-                y = jnp.dot(hbf[rows, :], wo[slot], preferred_element_type=F32).astype(BF)
-                obuf[pl.ds(e * (cap // 16), cap // 16)] = y.reshape(cap // 16, 16, wd)
 
                 @pl.when(s + NO < nch * nexp)
                 def _():
                     wo_copy(s + NO).start()
-            return 0
-
-        lax.fori_loop(0, nexp // 2, pair, 0)
+
         for q, r in enumerate(RETURN_ORDER):
             hacc[c * 4 + q] = combine(r + 1)
+        for q in range(4):
             d2d_copy(c, q).start()
         for q, r in enumerate(RETURN_ORDER):
-            y = combine(r)
+            mine[q] = combine(r)
+        for q, r in enumerate(RETURN_ORDER):
             d2d_copy(c, q).wait_recv()
-            y = y + d2d_in[c * 4 + q]
+            y = mine[q] + d2d_in[c * 4 + q]
             if r == 6:
                 out1[c, 0, 1] = y[:half].astype(BF)
                 out1[c, 1, 1] = y[half:].astype(BF)
@@ -436,6 +441,7 @@
                 pltpu.VMEM((nch, 2, half, wd), BF),
                 pltpu.VMEM((nch, 2, half, wd), F32),
                 pltpu.VMEM((nch, 2, half, wd), F32),
+                pltpu.VMEM((4, tok_dev, wd), F32),
                 pltpu.VMEM((nch, tok_dev, wd), BF),
                 pltpu.VMEM((8, ntok), F32),
                 pltpu.VMEM((ntok // 128, 32, 128), F32),

time: 95.7 us -> 84 us (0.88)
  Pallas kernels: 93.4 us -> 81.7 us
    pallas_call x1, Pallas kernels: 93.4 us -> 81.7 us  [device_fn(): pl.pallas_call(functools.partial(moe_kernel, cfg), out_shape=jax.ShapeDty...]
where the time goes in v4:
time: 84 us; the launch traced here: 83.8 us
  Pallas kernels  81.7 us (97%)
  local copies, waits for them, and re-layouts  2.09 us (2%)
    pallas_call x1, Pallas kernels, device_fn(): pl.pallas_call(functools.partial(moe_kernel, cfg), out_shape=jax.ShapeDty...  81.7 us
    unnamed x1, local copies, waits for them, and re-layouts  2.09 us

profile of v4, /device:TPU:0, one launch (start us, length us, event | category | flops | bytes accessed | tf_op | source)
XLA Modules:
  0.0 83.8 jit_solution(6924948685493632185)
XLA Ops:
  0.0 81.7 %shard_map.55 = bf16[192,2048]{1,0:T(8,128)(2,1)} custom-call(s32[8,192]{1,0:T(8,128)} %bitcast.2, f32[8,192]{1,0:T(8,128)} %bitcast.3, bf16[192,2048]{1,0:T(8,128)(2,1)} %tok_hbm.1, bf16[8,2048,1024]{2,1,0:T(8,128)(2,1)} %wi_hbm.1, bf16[8,1024,2048]{2,1,0:T(8,128)(2,1)} %wo_hbm.1), custom_call_target="tpu_custom_call" | custom-call | tf_op jit(solution)/shard_map/pallas_call | solution.py:421
  81.7 2.1 %copy.7 = bf16[192,2048]{1,0:T(8,128)(2,1)} copy(bf16[192,2048]{1,0:T(8,128)(2,1)} %shard_map.55) | data formatting | bytes 1572864
